TPU v7x, 256 devices: a 4x2x16 block of a 4x16x16 slice. The times are simulated.
256 devices in a mesh: grp: 2 (over y), seq: 64 (over x, z), head: 2 (over core).
Axes of the slice: x: 4, y: 2, z: 16, core: 2. Of those that a mesh axis runs over, the one named last changes fastest.
The devices are a block of a 4x16x16 slice.
Arguments:
- query_rows: bfloat16 [16, 32, 128], P('grp', 'head'), parts along dimension 0, may hold values from -100 to 100
- cache_keys: bfloat16 [4096, 8, 128, 128], P(('grp', 'seq'), 'head'), parts along dimension 0, may hold values from -5 to 5
- cache_values: bfloat16 [4096, 8, 128, 128], P(('grp', 'seq'), 'head'), parts along dimension 0, may hold values from -6 to 6
- page_table: int32 [4096], P('grp'), parts along dimension 0, may hold values from 0 to 2047, as said below
- seq_lengths: int32 [16], P('grp'), parts along dimension 0, may hold values from 128 to 32768, as said below
Outputs:
- attended: bfloat16 [16, 32, 128], P('grp', 'head'), parts along dimension 0
There are 2 independent parts, one for each index of `grp`. A program takes and returns all parts, laid end to end along the dimension named above; each array names one. Nothing has to cross between parts.
Inputs may be any that keep to these rules, and one draw needn't show every extreme that they name: `page_table`: entry b * 256 + j is the pool slot of page j of sequence b; slot s lies on index s // 32 of seq; every slot appears once. `seq_lengths`: some sequence has exactly 32768 tokens.
All inputs are finite; a program needn't handle non-finite values.
Results may differ from a plain program's by a relative error of at most 0.0029.
Values may be sent and summed in bfloat16 or wider, within the bound.
A program may use at most 64 MiB of HBM per device.

v0:
```python
import functools
import math

import jax
import jax.numpy as jnp
from jax import lax
from jax.sharding import Mesh
from jax.sharding import PartitionSpec as P

SEQ = ("seq_0", "seq_1")
GRP_SEQ = ("grp", "seq_0", "seq_1")


very_low = -1e30


def over_axes(value, axes):
    return functools.reduce(lax.pmax, axes, value)


def split_up(value, dim, peers):
    shape = value.shape
    blocks = value.reshape(*shape[:dim], peers, shape[dim] // peers, *shape[dim + 1 :])
    return jnp.moveaxis(blocks, dim, 0)


def sent_and_summed(value, axis, dim):
    blocks = split_up(value, dim, lax.axis_size(axis))
    arrived = lax.all_to_all(blocks, axis, split_axis=0, concat_axis=0, tiled=True)
    return arrived.sum(axis=0)


def sent_together(arrays, axis, dim, along):
    widths = [math.prod(a.shape[along:]) for a in arrays]
    both = jnp.concatenate(
        [a.reshape(*a.shape[:along], w) for a, w in zip(arrays, widths)], axis=along
    )
    filled = sent_and_summed(both, axis, dim)
    blocks = jnp.split(filled, [sum(widths[:k]) for k in range(1, len(widths))], axis=along)
    return tuple(
        (b.reshape(*filled.shape[:along], *a.shape[along:]) for a, b in zip(arrays, blocks))
    )


def copy_for_each(value, axis):
    peers = lax.axis_size(axis)
    return lax.all_to_all(
        jnp.broadcast_to(value[None], (peers, *value.shape)), axis, 0, 0, tiled=True
    )


def joined_along(blocks, dim):
    blocks = jnp.moveaxis(blocks, 0, dim)
    shape = blocks.shape
    return blocks.reshape(*shape[:dim], shape[dim] * shape[dim + 1], *shape[dim + 2 :])


def gathered_copies(value, axis, dim):
    blocks = copy_for_each(value, axis)
    return joined_along(blocks, dim)


def shards(query_rows, cache_keys, cache_values, page_table, seq_lengths):
    slot_count, kv_local, page_len, head_dim = cache_keys.shape
    batch_size, heads_local, _ = query_rows.shape
    group_size = heads_local // kv_local
    pool_size = page_table.shape[0]
    table_width = pool_size // batch_size
    score_scale = 1.0 / math.sqrt(head_dim)
    first_slot = lax.axis_index(SEQ) * slot_count
    slot_ids = first_slot + jnp.arange(slot_count, dtype=jnp.int32)
    matches = page_table[:, None] == slot_ids[None, :]
    entries = jnp.sum(
        jnp.where(matches, jnp.arange(pool_size, dtype=jnp.int32)[:, None], 0), axis=0
    )
    owners = entries // table_width
    logical = entries % table_width
    owner_hot = owners[:, None] == jnp.arange(batch_size, dtype=jnp.int32)[None, :]
    seq_len = jnp.sum(jnp.where(owner_hot, seq_lengths[None, :], 0), axis=1)
    positions = logical[:, None] * page_len + jnp.arange(page_len, dtype=jnp.int32)[None, :]
    live_mask = (positions < seq_len[:, None])[:, None, None, :]
    slot_query = jnp.take(query_rows, owners, axis=0).reshape(
        slot_count, kv_local, group_size, head_dim
    )
    scores = (
        jnp.einsum("sgqd,sgtd->sgqt", slot_query, cache_keys, preferred_element_type=jnp.float32)
        * score_scale
    )
    slot_top = jnp.max(jnp.where(live_mask, scores, very_low), axis=-1)
    local_top = jnp.max(jnp.where(owner_hot[:, :, None, None], slot_top[:, None], very_low), axis=0)
    row_top = over_axes(local_top.reshape(batch_size, heads_local), SEQ)
    slot_ref = jnp.take(row_top, owners, axis=0).reshape(slot_count, kv_local, group_size)
    weights = jnp.where(live_mask, jnp.exp(scores - slot_ref[..., None]), 0.0)
    slot_total = jnp.sum(weights, axis=-1).reshape(slot_count, heads_local)
    slot_numer = jnp.einsum(
        "sgqt,sgtd->sgqd",
        weights.astype(jnp.bfloat16),
        cache_values,
        preferred_element_type=jnp.float32,
    ).reshape(slot_count, heads_local, head_dim)
    owner_float = owner_hot.astype(jnp.float32)
    totals = jnp.einsum(
        "sb,sr->br", owner_float, slot_total, precision=lax.Precision.HIGHEST
    ).reshape(batch_size * heads_local)
    numerators = jnp.einsum(
        "sb,srd->brd", owner_float, slot_numer, precision=lax.Precision.HIGHEST
    ).reshape(batch_size * heads_local, head_dim)
    share_numer, share_total = sent_together((numerators, totals), SEQ, 0, 1)
    share_out = (share_numer / share_total[:, None]).astype(jnp.bfloat16)
    finished = gathered_copies(share_out, SEQ, 0)
    return finished.reshape(batch_size, heads_local, head_dim)


def solution(mesh):
    split = Mesh(
        mesh.devices.reshape(mesh.shape["grp"], 4, 16, mesh.shape["head"]),
        ("grp", "seq_0", "seq_1", "head"),
    )
    return jax.shard_map(
        shards,
        mesh=split,
        in_specs=(
            P("grp", "head", None),
            P(GRP_SEQ, "head", None, None),
            P(GRP_SEQ, "head", None, None),
            P("grp"),
            P("grp"),
        ),
        out_specs=P("grp", "head", None),
        check_vma=False,
    )
```

profile of v0, /device:TPU:40, one launch (start us, length us, event | category | flops | bytes accessed | tf_op | source)
XLA Modules:
  0.0 113.7 jit_solution(407009868676864819)
XLA Ops:
  0.0 0.0 copy-start
  0.0 0.9 select_reduce_fusion.1
  1.0 0.7 select_reduce_fusion.3
  1.7 0.1 add_compare_fusion
  1.8 0.0 copy-done
  1.8 0.6 gather_fusion
  2.4 4.6 %select_reduce_fusion = (f32[32,4,4]{2,1,0:T(4,128)S(1)}, f32[32,4,4,128]{3,2,1,0:T(4,128)S(1)}) fusion(pred[32,128]{1,0:T(8,128)(4,1)S(1)} %add_compare_fusion, bf16[32,4,128,128]{3,2,1,0:T(8,128)(2,1)} %param.6, bf16[32,4,4,128]{3,2,1,0:T(4,128)(2,1)S(1)} %bitcast.25, pred[32]{0:T(512)(128)(4,1)S(1)} %get-tuple-element.5), kind=kOutput, calls=%fused_computation.6 | convolution fusion | flops 17038848 | bytes 4593696 | tf_op jit(solution)/shard_map/sgqd,sgtd->sgqt/dot_general | solution.py:86
  7.0 0.1 copy.42
  7.1 0.1 select_reduce_fusion.2
  7.2 0.1 copy.43
  7.3 10.9 %pmax.14 = f32[8,16]{1,0:T(8,128)S(1)} all-reduce(f32[8,16]{1,0:T(8,128)S(1)} %copy.43), channel_id=1, replica_groups=mesh['grp'=2,'seq_0'=4,'seq_1'=16,'head'=2] {'seq_0'}, use_global_device_ids=true, to_apply=%region_4.5 | all-reduce | flops 128 | bytes 1024 | tf_op jit(solution)/shard_map/pmax | solution.py:18
  18.2 49.4 %pmax.15 = f32[8,16]{1,0:T(8,128)S(1)} all-reduce(f32[8,16]{1,0:T(8,128)S(1)} %pmax.14), channel_id=1, replica_groups=mesh['grp'=2,'seq_0'=4,'seq_1'=16,'head'=2] {'seq_1'}, use_global_device_ids=true, to_apply=%region_5.6 | all-reduce | flops 128 | bytes 1024 | tf_op jit(solution)/shard_map/pmax | solution.py:18
  67.6 0.6 gather_fusion.1
  68.2 0.1 copy.44
  68.3 0.1 copy.45
  68.4 0.4 fusion.2
  68.8 3.4 %fusion.4 = f32[32,4,4,128]{3,2,1,0:T(4,128)S(1)} fusion(bf16[32,4,128,128]{3,2,1,0:T(8,128)(2,1)} %param.7, f32[32,4,4,128]{3,2,1,0:T(4,128)S(1)} %get-tuple-element.8, f32[32,4,4]{2,1,0:T(4,128)S(1)} %copy.45, pred[32,128]{1,0:T(8,128)(4,1)S(1)} %add_compare_fusion), kind=kOutput, calls=%fused_computation.10 | convolution fusion | flops 16973824 | bytes 4724736 | tf_op jit(solution)/shard_map/sgqt,sgtd->sgqd/dot_general | solution.py:95
  72.3 0.1 copy.48
  72.4 0.1 fusion.13
  72.5 0.3 fusion
  72.8 0.1 concatenate.11
  73.0 0.1 pad_maximum_fusion
  73.0 19.5 %all_to_all.10 = f32[64,2,129]{2,1,0:T(2,128)S(1)} all-to-all(f32[64,2,129]{2,1,0:T(2,128)S(1)} %pad_maximum_fusion), channel_id=1, replica_groups=mesh['grp'=2,'seq_0'=4,'seq_1'=16,'head'=2] {'seq_0','seq_1'}, dimensions={0} | all-to-all | bytes 132096 | tf_op jit(solution)/shard_map/all_to_all | solution.py:29
  92.6 0.1 reduce_sum.42
  92.7 0.1 slice_reduce_fusion
  92.8 0.1 fusion.16
  92.9 20.2 %all_to_all.11 = bf16[64,2,128]{2,1,0:T(2,128)(2,1)S(1)} all-to-all(bf16[64,2,128]{2,1,0:T(2,128)(2,1)S(1)} %broadcast_in_dim.114), channel_id=1, replica_groups=mesh['grp'=2,'seq_0'=4,'seq_1'=16,'head'=2] {'seq_0','seq_1'}, dimensions={0} | all-to-all | bytes 65536 | tf_op jit(solution)/shard_map/all_to_all | solution.py:47
  113.1 0.6 copy.53
  (9 shorter events, 0.1 us)
Async XLA Ops:
  0.0 1.8 %copy-start = (bf16[8,16,128]{2,1,0:T(8,128)(2,1)S(1)}, bf16[8,16,128]{2,1,0:T(8,128)(2,1)}, u32[]{:S(2)}) copy-start(bf16[8,16,128]{2,1,0:T(8,128)(2,1)} %param.5) | copy-start | bytes 98308
where the time goes:
time: 114 us
  blocking collectives  100 us (88%)
  matrix products  8.46 us (7%)
  other arithmetic  2.57 us (2%)
  local copies, waits for them, and re-layouts  2.54 us (2%)
    pmax x2, blocking collectives, over_axes(): return functools.reduce(lax.pmax, axes, value)  60.3 us
    all_to_all x1, blocking collectives, copy_for_each(): lax.all_to_all(jnp.broadcast_to(value[None], (peers, *value.shape)), axis...  20.2 us
    all_to_all x1, blocking collectives, sent_and_summed(): lax.all_to_all(blocks, axis, split_axis=0, concat_axis=0, tiled=True)  19.5 us
    dot_general x1, matrix products, shards(): jnp.einsum('sgqd,sgtd->sgqt', slot_query, cache_keys, preferred_element_t...  4.6 us
    dot_general x1, matrix products, shards(): jnp.einsum('sgqt,sgtd->sgqd', weights.astype(jnp.bfloat16), cache_values,...  3.45 us

commit v1 on v0

v1 whole, which is shorter than its diff:
```python
import functools
import math

import jax
import jax.numpy as jnp
from jax import lax
from jax.experimental import pallas as pl
from jax.experimental.pallas import tpu as pltpu
from jax.sharding import PartitionSpec as P

MESH = pl.DeviceIdType.MESH
NX, NZ = 4, 16
PAIR = 2
VERY_LOW = -1e30


def remote(src, dst, send, recv, seq):
    return pltpu.make_async_remote_copy(
        src_ref=src,
        dst_ref=dst,
        send_sem=send,
        recv_sem=recv,
        device_id={"seq": seq},
        device_id_type=MESH,
    )


def to_column(row, rows):
    lane = lax.broadcasted_iota(jnp.int32, (rows, row.shape[1]), 1)
    sub = lax.broadcasted_iota(jnp.int32, (rows, row.shape[1]), 0)
    return jnp.sum(jnp.where(lane == sub, row, 0.0), axis=1, keepdims=True)


def merged(parts, rows):
    tops = [p[rows : rows + 1] for p in parts]
    top = functools.reduce(jnp.maximum, tops)
    total, numer = None, None
    for p, t in zip(parts, tops):
        factor = jnp.exp2(t - top)
        tot = p[rows + 1 : rows + 2] * factor
        num = p[:rows] * to_column(factor, rows)
        total = tot if total is None else total + tot
        numer = num if numer is None else numer + num
    return numer, top, total


def kernel(
    q_hbm, k_hbm, v_hbm, table_hbm, len_ref, out_ref,
    q_buf, q_f32, k_buf, v_buf, table_buf, bias, scores, probs,
    part, mid, share, recv1, recv2, recv3,
    load_sem, k_sem, v_sem, send1, sem1, send2, sem2, send3, sem3,
):
    slots, kv, page, dim = k_hbm.shape
    batch, heads, _ = q_hbm.shape
    group = heads // kv
    table_rows = table_hbm.shape[0] // batch
    rows = part.shape[1]

    load_q = pltpu.make_async_copy(q_hbm, q_buf, load_sem.at[0])
    load_t = pltpu.make_async_copy(table_hbm, table_buf, load_sem.at[1])
    load_q.start()
    load_t.start()
    loads_k = [pltpu.make_async_copy(k_hbm.at[:, g], k_buf.at[g], k_sem.at[g]) for g in range(kv)]
    loads_v = [pltpu.make_async_copy(v_hbm.at[:, g], v_buf.at[g], v_sem.at[g]) for g in range(kv)]
    for g in range(kv):
        loads_k[g].start()
        loads_v[g].start()

    me = lax.axis_index("seq")
    x, z = me // NZ, me % NZ
    peers = NX * PAIR
    mine = x * PAIR + z % PAIR
    z_base = (z // PAIR) * PAIR
    chunk = [(mine + i) % peers for i in range(peers)]
    near = [(c // PAIR) * NZ + z_base + c % PAIR for c in chunk]
    far = [x * NZ + (z + PAIR * i) % NZ for i in range(NZ // PAIR)]

    barrier = pltpu.get_barrier_semaphore()
    others = near[1:] + far[1:]
    for other in others:
        pl.semaphore_signal(barrier, inc=1, device_id={"seq": other}, device_id_type=MESH)

    load_t.wait()
    first = me * slots
    lane = lax.broadcasted_iota(jnp.int32, (batch, page), 1)
    sub = lax.broadcasted_iota(jnp.int32, (batch, page), 0)
    length = jnp.zeros((batch, page), jnp.int32)
    for b in range(batch):
        length = jnp.where(sub == b, len_ref[b], length)
    tables = [table_buf[pl.ds(r, batch, stride=table_rows), :] for r in range(table_rows)]
    spans = [(length - page * (lane + page * r)).astype(jnp.float32) for r in range(table_rows)]
    lane_f32 = lane.astype(jnp.float32)
    for s in range(slots):
        found = functools.reduce(
            jnp.add, [jnp.where(t == first + s, n, 0.0) for t, n in zip(tables, spans)]
        )
        live = jnp.sum(found, axis=1, keepdims=True)
        bias[s] = jnp.where(lane_f32 < live, 0.0, VERY_LOW)

    load_q.wait()
    q_f32[...] = q_buf[...].astype(jnp.float32).reshape(batch * heads, dim)

    factor = math.log2(math.e) / math.sqrt(dim)
    tops = jnp.zeros((batch, page), jnp.float32)
    totals = jnp.zeros((batch, page), jnp.float32)
    for g in range(kv):
        query = jnp.concatenate(
            [q_f32[pl.ds(group * g + i, batch, stride=heads), :] for i in range(group)], axis=0
        ).astype(jnp.bfloat16)
        loads_k[g].wait()
        best = None
        for s in range(0, slots, 2):
            keys = k_buf[g, s : s + 2].reshape(2 * page, dim)
            got = lax.dot_general(
                query, keys, (((1,), (1,)), ((), ())), preferred_element_type=jnp.float32
            )
            for u in range(2):
                add = jnp.concatenate([bias[s + u]] * group, axis=0)
                now = got[:, u * page : (u + 1) * page] * factor + add
                scores[:, (s + u) * page : (s + u + 1) * page] = now
                best = now if best is None else jnp.maximum(best, now)
        top = jnp.max(best, axis=1, keepdims=True)
        total = jnp.zeros((group * batch, page), jnp.float32)
        for s in range(slots):
            p = jnp.exp2(scores[:, s * page : (s + 1) * page] - top)
            total = total + p
            probs[:, s * page : (s + 1) * page] = p.astype(jnp.bfloat16)
        total = jnp.sum(total, axis=1, keepdims=True)
        loads_v[g].wait()
        numer = jnp.dot(
            probs[...], v_buf[g].reshape(slots * page, dim), preferred_element_type=jnp.float32
        )
        for i in range(group):
            h = group * g + i
            own = slice(i * batch, (i + 1) * batch)
            part[:, h, :] = numer[own]
            tops = jnp.where(lane == h, top[own], tops)
            totals = jnp.where(lane == h, total[own], totals)
    part[:, heads, :] = tops
    part[:, heads + 1, :] = totals

    pl.semaphore_wait(barrier, len(others))

    copies = [
        remote(part.at[chunk[i]], recv1.at[i - 1], send1.at[i - 1], sem1.at[i - 1], near[i])
        for i in range(1, peers)
    ]
    for c in copies:
        c.start()
    own = part[mine]
    for c in copies:
        c.wait_recv()
    numer, top, total = merged([own] + [recv1[i] for i in range(peers - 1)], heads)
    mid[0:heads] = numer
    mid[heads : heads + 1] = top
    mid[heads + 1 : heads + 2] = total

    copies2 = [
        remote(mid, recv2.at[i - 1], send2.at[i - 1], sem2.at[i - 1], far[i])
        for i in range(1, NZ // PAIR)
    ]
    for c in copies2:
        c.start()
    own = mid[...]
    for c in copies2:
        c.wait_recv()
    numer, top, total = merged([own] + [recv2[i] for i in range(NZ // PAIR - 1)], heads)
    share[...] = (numer / to_column(total, heads)).astype(jnp.bfloat16)

    copies3 = [
        remote(share, recv3.at[i - 1], send3.at[i - 1], sem3.at[i - 1], near[i])
        for i in range(1, peers)
    ]
    for c in copies3:
        c.start()
    out_ref[mine] = share[...]
    for i, c in enumerate(copies3):
        c.wait_recv()
        out_ref[(mine + peers - 1 - i) % peers] = recv3[i]
    for c in copies + copies2 + copies3:
        c.wait_send()


def shards(query_rows, cache_keys, cache_values, page_table, seq_lengths):
    slots, kv, page, dim = cache_keys.shape
    batch, heads, _ = query_rows.shape
    peers, fars = NX * PAIR, NZ // PAIR
    rows = heads + 8
    dma = pltpu.SemaphoreType.DMA
    return pl.pallas_call(
        kernel,
        out_shape=jax.ShapeDtypeStruct(query_rows.shape, query_rows.dtype),
        in_specs=[pl.BlockSpec(memory_space=pl.ANY)] * 4
        + [pl.BlockSpec(memory_space=pltpu.SMEM)],
        out_specs=pl.BlockSpec(memory_space=pltpu.VMEM),
        scratch_shapes=[
            pltpu.VMEM(query_rows.shape, query_rows.dtype),
            pltpu.VMEM((batch * heads, dim), jnp.float32),
            pltpu.VMEM((kv, slots, page, dim), cache_keys.dtype),
            pltpu.VMEM((kv, slots, page, dim), cache_values.dtype),
            pltpu.VMEM((page_table.shape[0] // page, page), jnp.int32),
            pltpu.VMEM((slots, batch, page), jnp.float32),
            pltpu.VMEM((heads // kv * batch, slots * page), jnp.float32),
            pltpu.VMEM((heads // kv * batch, slots * page), jnp.bfloat16),
            pltpu.VMEM((batch, rows, dim), jnp.float32),
            pltpu.VMEM((rows, dim), jnp.float32),
            pltpu.VMEM((heads, dim), jnp.bfloat16),
            pltpu.VMEM((peers - 1, rows, dim), jnp.float32),
            pltpu.VMEM((fars - 1, rows, dim), jnp.float32),
            pltpu.VMEM((peers - 1, heads, dim), jnp.bfloat16),
            dma((2,)),
            dma((kv,)),
            dma((kv,)),
            dma((peers - 1,)),
            dma((peers - 1,)),
            dma((fars - 1,)),
            dma((fars - 1,)),
            dma((peers - 1,)),
            dma((peers - 1,)),
        ],
        compiler_params=pltpu.CompilerParams(collective_id=0, has_side_effects=True),
        name="attend",
    )(query_rows, cache_keys, cache_values, page_table.reshape(-1, page), seq_lengths)


def solution(mesh):
    return jax.shard_map(
        shards,
        mesh=mesh,
        in_specs=(
            P("grp", "head", None),
            P(("grp", "seq"), "head", None, None),
            P(("grp", "seq"), "head", None, None),
            P("grp"),
            P("grp"),
        ),
        out_specs=P("grp", "head", None),
        check_vma=False,
    )
```

time: 114 us -> 46 us (0.40)
  blocking collectives: 100 us -> 0 us
  Pallas kernels: 0 us -> 44.5 us
  matrix products: 8.46 us -> 0 us
  other arithmetic: 2.57 us -> 0 us
  local copies, waits for them, and re-layouts: 2.54 us -> 1.38 us
    pmax x2 -> x0, blocking collectives: 60.3 us -> none  [over_axes(): return functools.reduce(lax.pmax, axes, value)]
    pallas_call x0 -> x1, Pallas kernels: none -> 44.5 us  [shards(): pl.pallas_call(kernel, out_shape=jax.ShapeDtypeStruct(query_rows.shape, q...]
    all_to_all x2 -> x0, blocking collectives: 39.7 us -> none  [the longest x1 20.2 us: copy_for_each(): lax.all_to_all(jnp.broadcast_to(value[None], (peers, *value.shape)), axis...]
    dot_general x4 -> x0, matrix products: 8.46 us -> none  [the longest x1 4.6 us: shards(): jnp.einsum('sgqd,sgtd->sgqt', slot_query, cache_keys, preferred_element_t...]
    reduce_sum x4 -> x0, other arithmetic: 2.19 us -> none  [the longest x1 0.91 us: shards(): jnp.sum(jnp.where(matches, jnp.arange(pool_size, dtype=jnp.int32)[:, None...]
    gather x3 -> x0, local copies, waits for them, and re-layouts: 1.23 us -> none  [the longest x2 0.64 us: shards(): jnp.take(row_top, owners, axis=0).reshape(slot_count, kv_local, group_size)]
where the time goes in v1:
time: 46 us; the launch traced here: 45.8 us
  Pallas kernels  44.5 us (97%)
  local copies, waits for them, and re-layouts  1.38 us (3%)
    pallas_call x1, Pallas kernels, shards(): pl.pallas_call(kernel, out_shape=jax.ShapeDtypeStruct(query_rows.shape, q...  44.5 us
    unnamed x1, local copies, waits for them, and re-layouts  1.38 us

profile of v1, /device:TPU:40, one launch (start us, length us, event | category | flops | bytes accessed | tf_op | source)
XLA Modules:
  0.0 45.8 jit_solution(1397066421783810007)
XLA Ops:
  0.0 44.5 %attend.1 = bf16[8,16,128]{2,1,0:T(8,128)(2,1)} custom-call(bf16[8,16,128]{2,1,0:T(8,128)(2,1)} %q_hbm.1, bf16[32,4,128,128]{3,2,1,0:T(8,128)(2,1)} %k_hbm.1, bf16[32,4,128,128]{3,2,1,0:T(8,128)(2,1)} %v_hbm.1, s32[16,128]{1,0:T(8,128)} %bitcast.1, s32[8]{0:T(128)} %len_ref.1), custom_call_target="tpu_custom_call" | custom-call | tf_op jit(solution)/shard_map/attend/pallas_call | solution.py:190
  44.5 1.4 %copy.7 = bf16[8,16,128]{2,1,0:T(8,128)(2,1)} copy(bf16[8,16,128]{2,1,0:T(8,128)(2,1)} %attend.1) | data formatting | bytes 65536

commit v2 on v1

v2 whole, which is shorter than its diff:
```python
import functools
import math

import jax
import jax.numpy as jnp
from jax import lax
from jax.experimental import pallas as pl
from jax.experimental.pallas import tpu as pltpu
from jax.sharding import PartitionSpec as P

MESH = pl.DeviceIdType.MESH
NX, NZ = 4, 16
LATE = 12
VERY_LOW = -1e30
LEVELS = 32767.0


def remote(src, dst, send, recv, seq):
    return pltpu.make_async_remote_copy(
        src_ref=src,
        dst_ref=dst,
        send_sem=send,
        recv_sem=recv,
        device_id={"seq": seq},
        device_id_type=MESH,
    )


def diagonal(rows, lanes, first):
    lane = lax.broadcasted_iota(jnp.int32, (rows, lanes), 1)
    sub = lax.broadcasted_iota(jnp.int32, (rows, lanes), 0)
    return lane == sub + first


def to_column(row, rows):
    return jnp.sum(jnp.where(diagonal(rows, row.shape[1], 0), row, 0.0), axis=1, keepdims=True)


def kernel(
    q_hbm, k_hbm, v_hbm, table_hbm, len_ref, out_ref,
    q_buf, q_f32, k_buf, v_buf, table_buf, bias, scores, probs,
    numer16, stats, recv16, recv_stats, total_numer, total_row, top_row, finished, fin_f32,
    load_sem, k_sem, v_sem, send_n, send_s, recv_n, recv_s, send_f, recv_f,
):
    slots, kv, page, dim = k_hbm.shape
    batch, heads, _ = q_hbm.shape
    group = heads // kv
    table_rows = table_hbm.shape[0] // batch
    rows = group * batch

    load_q = pltpu.make_async_copy(q_hbm, q_buf, load_sem.at[0])
    load_t = pltpu.make_async_copy(table_hbm, table_buf, load_sem.at[1])
    load_q.start()
    load_t.start()
    loads_k = [pltpu.make_async_copy(k_hbm.at[:, g], k_buf.at[g], k_sem.at[g]) for g in range(kv)]
    loads_v = [pltpu.make_async_copy(v_hbm.at[:, g], v_buf.at[g], v_sem.at[g]) for g in range(kv)]
    for g in range(kv):
        loads_k[g].start()
        loads_v[g].start()

    me = lax.axis_index("seq")
    mine, z = me // NZ, me % NZ
    owner = z == 0
    owners = [g * NZ for g in range(kv)]

    barrier = pltpu.get_barrier_semaphore()

    @pl.when(owner)
    def _():
        @pl.loop(1, NX * NZ)
        def _(i):
            other = (me + i) % (NX * NZ)
            pl.semaphore_signal(barrier, inc=1, device_id={"seq": other}, device_id_type=MESH)

    @pl.when(jnp.logical_not(owner))
    def _():
        for other in owners:
            pl.semaphore_signal(barrier, inc=1, device_id={"seq": other}, device_id_type=MESH)

    load_t.wait()
    first = me * slots
    lane = lax.broadcasted_iota(jnp.int32, (batch, page), 1)
    sub = lax.broadcasted_iota(jnp.int32, (batch, page), 0)
    length = jnp.zeros((batch, page), jnp.int32)
    for b in range(batch):
        length = jnp.where(sub == b, len_ref[b], length)
    tables = [table_buf[pl.ds(r, batch, stride=table_rows), :] for r in range(table_rows)]
    spans = [(length - page * (lane + page * r)).astype(jnp.float32) for r in range(table_rows)]
    lane_f32 = lane.astype(jnp.float32)
    for s in range(slots):
        found = functools.reduce(
            jnp.add, [jnp.where(t == first + s, n, 0.0) for t, n in zip(tables, spans)]
        )
        live = jnp.sum(found, axis=1, keepdims=True)
        bias[s] = jnp.where(lane_f32 < live, 0.0, VERY_LOW)

    load_q.wait()
    q_f32[...] = q_buf[...].astype(jnp.float32).reshape(batch * heads, dim)

    factor = math.log2(math.e) / math.sqrt(dim)

    def sends(g):
        return (
            remote(numer16.at[g], recv16.at[me], send_n.at[g], recv_n.at[me], owners[g]),
            remote(stats.at[g], recv_stats.at[me], send_s.at[g], recv_s.at[me], owners[g]),
        )

    @pl.when(jnp.logical_not(owner))
    def _():
        pl.semaphore_wait(barrier, NX)

    for g in range(kv):
        query = jnp.concatenate(
            [q_f32[pl.ds(group * g + i, batch, stride=heads), :] for i in range(group)], axis=0
        ).astype(jnp.bfloat16)
        loads_k[g].wait()
        best = None
        for s in range(0, slots, 2):
            keys = k_buf[g, s : s + 2].reshape(2 * page, dim)
            got = lax.dot_general(
                query, keys, (((1,), (1,)), ((), ())), preferred_element_type=jnp.float32
            )
            for u in range(2):
                add = jnp.concatenate([bias[s + u]] * group, axis=0)
                now = got[:, u * page : (u + 1) * page] * factor + add
                scores[:, (s + u) * page : (s + u + 1) * page] = now
                best = now if best is None else jnp.maximum(best, now)
        top = jnp.max(best, axis=1, keepdims=True)
        total = jnp.zeros((rows, page), jnp.float32)
        for s in range(slots):
            p = jnp.exp2(scores[:, s * page : (s + 1) * page] - top)
            total = total + p
            probs[:, s * page : (s + 1) * page] = p.astype(jnp.bfloat16)
        total = jnp.sum(total, axis=1, keepdims=True)
        loads_v[g].wait()
        numer = jnp.dot(
            probs[...], v_buf[g].reshape(slots * page, dim), preferred_element_type=jnp.float32
        )
        largest = jnp.max(jnp.abs(numer), axis=1, keepdims=True)
        steps = numer * (LEVELS / jnp.maximum(largest, 1e-30))
        numer16[g] = jnp.floor(steps + 0.5).astype(jnp.int32).astype(jnp.int16)
        row = sum(
            jnp.where(diagonal(rows, dim, i * rows), column, 0.0)
            for i, column in enumerate((top, total, largest * (1.0 / LEVELS)))
        )
        stats[g] = jnp.sum(row, axis=0, keepdims=True)

        @pl.when(jnp.logical_not(owner))
        def _():
            for c in sends(g):
                c.start()

    @pl.when(owner)
    def _():
        pl.semaphore_wait(barrier, NX * NZ - 1)
        for g in range(kv):

            @pl.when(mine != g)
            def _():
                for c in sends(g):
                    c.start()

        recv16[me] = numer16[mine]
        recv_stats[me] = stats[mine]
        total_numer[...] = jnp.zeros_like(total_numer)
        total_row[...] = jnp.zeros_like(total_row)
        top_row[...] = jnp.full_like(top_row, VERY_LOW)

        def add(zz):
            sources = [xx * NZ + zz for xx in range(NX)]
            for src in sources:

                @pl.when(src != me)
                def _():
                    remote(numer16.at[0], recv16.at[src], send_n.at[0], recv_n.at[src], 0).wait_recv()
                    remote(stats.at[0], recv_stats.at[src], send_s.at[0], recv_s.at[src], 0).wait_recv()

            got = jnp.concatenate([recv_stats[src] for src in sources] * 2, axis=0)
            totals = pltpu.roll(got, dim - rows, 1)
            scales = pltpu.roll(got, dim - 2 * rows, 1)
            before = top_row[...]
            top = jnp.maximum(before, jnp.max(got, axis=0, keepdims=True))
            weight = jnp.exp2(got - top)
            keep = jnp.exp2(before - top)
            top_row[...] = top
            both = weight * totals
            new_total = total_row[...] * keep
            for i in range(NX):
                new_total = new_total + both[i : i + 1]
            total_row[...] = new_total
            scaled = weight * scales
            numer = total_numer[...] * to_column(keep, rows)
            for i, src in enumerate(sources):
                numer = numer + recv16[src].astype(jnp.int32).astype(jnp.float32) * to_column(
                    scaled[i : i + 1], rows
                )
            total_numer[...] = numer

        @pl.loop(1, LATE)
        def _(zz):
            add(zz)

        add(0)

        @pl.loop(LATE, NZ)
        def _(zz):
            add(zz)

        done = total_numer[...] / to_column(total_row[...], rows)
        finished[mine] = done.astype(finished.dtype)

        @pl.loop(0, NZ)
        def _(zz):
            for xx in range(NX):
                other = xx * NZ + zz

                @pl.when(other != me)
                def _():
                    remote(
                        finished.at[mine], finished.at[mine], send_f.at[other], recv_f.at[mine], other
                    ).start()

    for g in range(kv):

        @pl.when(me != owners[g])
        def _():
            remote(finished.at[g], finished.at[g], send_f.at[0], recv_f.at[g], 0).wait_recv()

    fin_f32[...] = finished[...].astype(jnp.float32).reshape(heads * batch, dim)
    for b in range(batch):
        out_ref[b] = fin_f32[pl.ds(b, heads, stride=batch), :].astype(out_ref.dtype)

    for g in range(kv):

        @pl.when(me != owners[g])
        def _():
            for c in sends(g):
                c.wait_send()

    @pl.when(owner)
    def _():
        @pl.loop(0, NX * NZ)
        def _(other):
            @pl.when(other != me)
            def _():
                remote(
                    finished.at[mine], finished.at[mine], send_f.at[other], recv_f.at[mine], other
                ).wait_send()


def shards(query_rows, cache_keys, cache_values, page_table, seq_lengths):
    slots, kv, page, dim = cache_keys.shape
    batch, heads, _ = query_rows.shape
    rows = heads // kv * batch
    devices = NX * NZ
    dma = pltpu.SemaphoreType.DMA
    return pl.pallas_call(
        kernel,
        out_shape=jax.ShapeDtypeStruct(query_rows.shape, query_rows.dtype),
        in_specs=[pl.BlockSpec(memory_space=pltpu.HBM)] * 4
        + [pl.BlockSpec(memory_space=pltpu.SMEM)],
        out_specs=pl.BlockSpec(memory_space=pltpu.VMEM),
        scratch_shapes=[
            pltpu.VMEM(query_rows.shape, query_rows.dtype),
            pltpu.VMEM((batch * heads, dim), jnp.float32),
            pltpu.VMEM((kv, slots, page, dim), cache_keys.dtype),
            pltpu.VMEM((kv, slots, page, dim), cache_values.dtype),
            pltpu.VMEM((page_table.shape[0] // page, page), jnp.int32),
            pltpu.VMEM((slots, batch, page), jnp.float32),
            pltpu.VMEM((rows, slots * page), jnp.float32),
            pltpu.VMEM((rows, slots * page), jnp.bfloat16),
            pltpu.VMEM((kv, rows, dim), jnp.int16),
            pltpu.VMEM((kv, 1, dim), jnp.float32),
            pltpu.VMEM((devices, rows, dim), jnp.int16),
            pltpu.VMEM((devices, 1, dim), jnp.float32),
            pltpu.VMEM((rows, dim), jnp.float32),
            pltpu.VMEM((1, dim), jnp.float32),
            pltpu.VMEM((1, dim), jnp.float32),
            pltpu.VMEM((kv, rows, dim), query_rows.dtype),
            pltpu.VMEM((heads * batch, dim), jnp.float32),
            dma((2,)),
            dma((kv,)),
            dma((kv,)),
            dma((kv,)),
            dma((kv,)),
            dma((devices,)),
            dma((devices,)),
            dma((devices,)),
            dma((kv,)),
        ],
        compiler_params=pltpu.CompilerParams(
            collective_id=0, has_side_effects=True, vmem_limit_bytes=56 << 20
        ),
        name="attend",
    )(query_rows, cache_keys, cache_values, page_table.reshape(-1, page), seq_lengths)


def solution(mesh):
    return jax.shard_map(
        shards,
        mesh=mesh,
        in_specs=(
            P("grp", "head", None),
            P(("grp", "seq"), "head", None, None),
            P(("grp", "seq"), "head", None, None),
            P("grp"),
            P("grp"),
        ),
        out_specs=P("grp", "head", None),
        check_vma=False,
    )
```

time: 46 us -> 48.2 us (1.048)
  the two profiles are of different devices: /device:TPU:40 before, /device:TPU:38 now
where the time goes in v2:
time: 48.2 us; the launch traced here: 48 us
  Pallas kernels  46.6 us (97%)
  local copies, waits for them, and re-layouts  1.38 us (3%)
    pallas_call x1, Pallas kernels, shards(): pl.pallas_call(kernel, out_shape=jax.ShapeDtypeStruct(query_rows.shape, q...  46.6 us
    unnamed x1, local copies, waits for them, and re-layouts  1.38 us

profile of v2, /device:TPU:38, one launch (start us, length us, event | category | flops | bytes accessed | tf_op | source)
XLA Modules:
  0.0 48.0 jit_solution(3139123312977803283)
XLA Ops:
  0.0 46.6 %attend.1 = bf16[8,16,128]{2,1,0:T(8,128)(2,1)} custom-call(bf16[8,16,128]{2,1,0:T(8,128)(2,1)} %q_hbm.1, bf16[32,4,128,128]{3,2,1,0:T(8,128)(2,1)} %k_hbm.1, bf16[32,4,128,128]{3,2,1,0:T(8,128)(2,1)} %v_hbm.1, s32[16,128]{1,0:T(8,128)} %bitcast.1, s32[8]{0:T(128)} %len_ref.1), custom_call_target="tpu_custom_call" | custom-call | tf_op jit(solution)/shard_map/attend/pallas_call | solution.py:257
  46.6 1.4 %copy.7 = bf16[8,16,128]{2,1,0:T(8,128)(2,1)} copy(bf16[8,16,128]{2,1,0:T(8,128)(2,1)} %attend.1) | data formatting | bytes 65536

commit v3 on v2

v3 whole, which is shorter than its diff:
```python
import functools
import math

import jax
import jax.numpy as jnp
from jax import lax
from jax.experimental import pallas as pl
from jax.experimental.pallas import tpu as pltpu
from jax.sharding import PartitionSpec as P

MESH = pl.DeviceIdType.MESH
NX, NZ = 4, 16
OWNER = 1
NEAR = 3
RELAY = 5
LATE = 13
VERY_LOW = -1e30
LEVELS = 32767.0


def remote(src, dst, send, recv, seq):
    return pltpu.make_async_remote_copy(
        src_ref=src,
        dst_ref=dst,
        send_sem=send,
        recv_sem=recv,
        device_id={"seq": seq},
        device_id_type=MESH,
    )


def diagonal(rows, lanes, first):
    lane = lax.broadcasted_iota(jnp.int32, (rows, lanes), 1)
    sub = lax.broadcasted_iota(jnp.int32, (rows, lanes), 0)
    return lane == sub + first


def to_column(row, rows):
    return jnp.sum(jnp.where(diagonal(rows, row.shape[1], 0), row, 0.0), axis=1, keepdims=True)


def kernel(
    q_hbm, k_hbm, v_hbm, table_hbm, len_hbm, out_ref,
    len_buf, q_buf, q_f32, k_buf, v_buf, table_buf, bias, scores, probs,
    numer16, stats, recv16, recv_stats, total_numer, total_row, top_row, finished, fin_f32,
    load_sem, k_sem, v_sem, send_n, send_s, recv_n, recv_s, send_f, recv_f, send_w, recv_w, ready,
):
    slots, kv, page, dim = k_hbm.shape
    batch, heads, _ = q_hbm.shape
    group = heads // kv
    table_rows = table_hbm.shape[0] // batch
    rows = group * batch
    pairs = [(g, g + 1) for g in range(0, kv, 2)]
    devices = NX * NZ

    load_t = pltpu.make_async_copy(table_hbm, table_buf, load_sem.at[0])
    load_l = pltpu.make_async_copy(len_hbm, len_buf, load_sem.at[1])
    load_q = pltpu.make_async_copy(q_hbm, q_buf, load_sem.at[2])
    loads_k = [pltpu.make_async_copy(k_hbm.at[:, g], k_buf.at[g], k_sem.at[g]) for g in range(kv)]
    loads_v = [pltpu.make_async_copy(v_hbm.at[:, g], v_buf.at[g], v_sem.at[g]) for g in range(kv)]
    load_t.start()
    load_l.start()
    load_q.start()
    for c in loads_k:
        c.start()

    me = lax.axis_index("seq")
    x, z = me // NZ, me % NZ
    owner = z == OWNER
    relay = z == RELAY
    fed = jnp.logical_and(z > NEAR, jnp.logical_not(relay))
    owners = [g * NZ + OWNER for g in range(kv)]
    column = [zz for zz in range(NEAR + 1, NZ) if zz != RELAY]

    barrier = pltpu.get_barrier_semaphore()

    def signal(sem, other):
        pl.semaphore_signal(sem, inc=1, device_id={"seq": other}, device_id_type=MESH)

    @pl.when(owner)
    def _():
        @pl.loop(1, devices)
        def _(i):
            signal(barrier, (me + i) % devices)

    @pl.when(jnp.logical_not(owner))
    def _():
        for other in owners:
            signal(barrier, other)

    @pl.when(relay)
    def _():
        for zz in column:
            signal(barrier, x * NZ + zz)

    with jax.named_scope("tw"):
        load_t.wait()
        load_l.wait()
        load_q.wait()
    for c in loads_v:
        c.start()
    first = me * slots
    lane = lax.broadcasted_iota(jnp.int32, (batch, page), 1)
    sub = lax.broadcasted_iota(jnp.int32, (batch, page), 0)
    length = jnp.zeros((batch, page), jnp.int32)
    for b in range(batch):
        length = jnp.where(sub == b, len_buf[b], length)
    tables = [table_buf[pl.ds(r, batch, stride=table_rows), :] for r in range(table_rows)]
    spans = [(length - page * (lane + page * r)).astype(jnp.float32) for r in range(table_rows)]
    lane_f32 = lane.astype(jnp.float32)
    for s in range(slots):
        found = functools.reduce(
            jnp.add, [jnp.where(t == first + s, n, 0.0) for t, n in zip(tables, spans)]
        )
        live = jnp.sum(found, axis=1, keepdims=True)
        bias[s] = jnp.where(lane_f32 < live, 0.0, VERY_LOW)
    q_f32[...] = q_buf[...].astype(jnp.float32).reshape(batch * heads, dim)

    factor = math.log2(math.e) / math.sqrt(dim)

    def sends(g):
        return (
            remote(numer16.at[g], recv16.at[me], send_n.at[g], recv_n.at[me], owners[g]),
            remote(stats.at[g], recv_stats.at[me], send_s.at[g], recv_s.at[me], owners[g]),
        )

    columns = []
    for p, pair in enumerate(pairs):
        blocks = []
        for i, g in enumerate(pair):
            query = jnp.concatenate(
                [q_f32[pl.ds(group * g + j, batch, stride=heads), :] for j in range(group)], axis=0
            ).astype(jnp.bfloat16)
            empty = jnp.zeros_like(query)
            blocks.append(jnp.concatenate([empty] * i + [query] + [empty] * (1 - i), axis=1))
        query = jnp.concatenate(blocks, axis=0)
        with jax.named_scope(f"kw{p}"):
            for g in pair:
                loads_k[g].wait()
        best = None
        for s in range(0, slots, 2):
            keys = jnp.concatenate(
                [k_buf[g, s : s + 2].reshape(2 * page, dim) for g in pair], axis=1
            )
            got = lax.dot_general(
                query, keys, (((1,), (1,)), ((), ())), preferred_element_type=jnp.float32
            )
            for u in range(2):
                add = jnp.concatenate([bias[s + u]] * (2 * group), axis=0)
                now = got[:, u * page : (u + 1) * page] * factor + add
                scores[p, :, (s + u) * page : (s + u + 1) * page] = now
                best = now if best is None else jnp.maximum(best, now)
        top = jnp.max(best, axis=1, keepdims=True)
        total = jnp.zeros((2 * rows, page), jnp.float32)
        for s in range(slots):
            w = jnp.exp2(scores[p, :, s * page : (s + 1) * page] - top)
            total = total + w
            probs[p, :, s * page : (s + 1) * page] = w.astype(jnp.bfloat16)
        columns.append((top, jnp.sum(total, axis=1, keepdims=True)))

    with jax.named_scope("bw"):

        @pl.when(fed)
        def _():
            pl.semaphore_wait(barrier, kv + 1)
            signal(ready, x * NZ + RELAY)

        @pl.when(jnp.logical_not(jnp.logical_or(owner, fed)))
        def _():
            pl.semaphore_wait(barrier, kv)

    for p, pair in enumerate(pairs):
        with jax.named_scope(f"vw{p}"):
            for g in pair:
                loads_v[g].wait()
        numers = jnp.zeros((2 * rows, 2 * dim), jnp.float32)
        for s in range(0, slots, 2):
            values = jnp.concatenate(
                [v_buf[g, s : s + 2].reshape(2 * page, dim) for g in pair], axis=1
            )
            numers = numers + jnp.dot(
                probs[p, :, s * page : (s + 2) * page], values, preferred_element_type=jnp.float32
            )
        for i, g in enumerate(pair):
            own = slice(i * rows, (i + 1) * rows)
            numer = numers[own, i * dim : (i + 1) * dim]
            largest = jnp.max(jnp.abs(numer), axis=1, keepdims=True)
            steps = numer * (LEVELS / jnp.maximum(largest, 1e-30))
            numer16[g] = jnp.floor(steps + 0.5).astype(jnp.int32).astype(jnp.int16)
            top, total = columns[p]
            row = sum(
                jnp.where(diagonal(rows, dim, j * rows), c, 0.0)
                for j, c in enumerate((top[own], total[own], largest * (1.0 / LEVELS)))
            )
            stats[g] = jnp.sum(row, axis=0, keepdims=True)

        @pl.when(jnp.logical_not(owner))
        def _():
            with jax.named_scope(f"snd{p}"):
                for g in pair:
                    for c in sends(g):
                        c.start()

    def near(zz, xx):
        other = xx * NZ + zz
        return remote(
            finished.at[x], finished.at[x], send_f.at[xx * (NEAR + 2) + min(zz, NEAR + 1)], recv_f.at[x], other
        )

    near_z = [OWNER] + [zz for zz in range(NEAR + 1) if zz != OWNER] + [RELAY]

    @pl.when(owner)
    def _():
        with jax.named_scope("bar"):
            pl.semaphore_wait(barrier, devices - 1)
        for g in range(kv):

            @pl.when(x != g)
            def _():
                for c in sends(g):
                    c.start()

        recv16[me] = numer16[x]
        recv_stats[me] = stats[x]
        total_numer[...] = jnp.zeros_like(total_numer)
        total_row[...] = jnp.zeros_like(total_row)
        top_row[...] = jnp.full_like(top_row, VERY_LOW)

        def add(zz):
            sources = [xx * NZ + zz for xx in range(NX)]
            with jax.named_scope("rw"):
                for src in sources:

                    @pl.when(src != me)
                    def _():
                        remote(numer16.at[0], recv16.at[src], send_n.at[0], recv_n.at[src], 0).wait_recv()
                        remote(stats.at[0], recv_stats.at[src], send_s.at[0], recv_s.at[src], 0).wait_recv()

            got = jnp.concatenate([recv_stats[src] for src in sources] * 2, axis=0)
            totals = pltpu.roll(got, dim - rows, 1)
            scales = pltpu.roll(got, dim - 2 * rows, 1)
            before = top_row[...]
            top = jnp.maximum(before, jnp.max(got, axis=0, keepdims=True))
            weight = jnp.exp2(got - top)
            keep = jnp.exp2(before - top)
            top_row[...] = top
            both = weight * totals
            new_total = total_row[...] * keep
            for i in range(NX):
                new_total = new_total + both[i : i + 1]
            total_row[...] = new_total
            scaled = weight * scales
            numer = total_numer[...] * to_column(keep, rows)
            for i, src in enumerate(sources):
                numer = numer + recv16[src].astype(jnp.int32).astype(jnp.float32) * to_column(
                    scaled[i : i + 1], rows
                )
            total_numer[...] = numer

        @pl.loop(OWNER + 1, LATE)
        def _(zz):
            add(zz)

        @pl.loop(0, OWNER + 1)
        def _(zz):
            add(OWNER - zz)

        @pl.loop(LATE, NZ)
        def _(zz):
            add(zz)

        done = total_numer[...] / to_column(total_row[...], rows)
        finished[x] = done.astype(finished.dtype)
        with jax.named_scope("bcast"):
            for zz in near_z:
                for xx in range(NX):
                    if zz == OWNER:

                        @pl.when(x != xx)
                        def _():
                            near(zz, xx).start()
                    else:
                        near(zz, xx).start()

    @pl.when(jnp.logical_not(fed))
    def _():
        for g in range(kv):

            @pl.when(me != owners[g])
            def _():
                with jax.named_scope(f"fw{g}"):
                    remote(finished.at[g], finished.at[g], send_f.at[0], recv_f.at[g], 0).wait_recv()

    def forward(i):
        return remote(finished, finished, send_w.at[i], recv_w, x * NZ + column[i])

    @pl.when(fed)
    def _():
        with jax.named_scope("fww"):
            forward(0).wait_recv()

    @pl.when(relay)
    def _():
        pl.semaphore_wait(ready, len(column))
        for i in range(len(column)):
            forward(i).start()

    fin_f32[...] = finished[...].astype(jnp.float32).reshape(heads * batch, dim)
    for b in range(batch):
        out_ref[b] = fin_f32[pl.ds(b, heads, stride=batch), :].astype(out_ref.dtype)

    with jax.named_scope("ws"):
        for g in range(kv):

            @pl.when(me != owners[g])
            def _():
                for c in sends(g):
                    c.wait_send()

        @pl.when(owner)
        def _():
            for zz in near_z:
                for xx in range(NX):
                    if zz == OWNER:

                        @pl.when(x != xx)
                        def _():
                            near(zz, xx).wait_send()
                    else:
                        near(zz, xx).wait_send()

        @pl.when(relay)
        def _():
            for i in range(len(column)):
                forward(i).wait_send()


def shards(query_rows, cache_keys, cache_values, page_table, seq_lengths):
    slots, kv, page, dim = cache_keys.shape
    batch, heads, _ = query_rows.shape
    rows = heads // kv * batch
    devices = NX * NZ
    dma = pltpu.SemaphoreType.DMA
    return pl.pallas_call(
        kernel,
        out_shape=jax.ShapeDtypeStruct(query_rows.shape, query_rows.dtype),
        in_specs=[pl.BlockSpec(memory_space=pltpu.HBM)] * 5,
        out_specs=pl.BlockSpec(memory_space=pltpu.VMEM),
        scratch_shapes=[
            pltpu.SMEM(seq_lengths.shape, seq_lengths.dtype),
            pltpu.VMEM(query_rows.shape, query_rows.dtype),
            pltpu.VMEM((batch * heads, dim), jnp.float32),
            pltpu.VMEM((kv, slots, page, dim), cache_keys.dtype),
            pltpu.VMEM((kv, slots, page, dim), cache_values.dtype),
            pltpu.VMEM((page_table.shape[0] // page, page), jnp.int32),
            pltpu.VMEM((slots, batch, page), jnp.float32),
            pltpu.VMEM((kv // 2, 2 * rows, slots * page), jnp.float32),
            pltpu.VMEM((kv // 2, 2 * rows, slots * page), jnp.bfloat16),
            pltpu.VMEM((kv, rows, dim), jnp.int16),
            pltpu.VMEM((kv, 1, dim), jnp.float32),
            pltpu.VMEM((devices, rows, dim), jnp.int16),
            pltpu.VMEM((devices, 1, dim), jnp.float32),
            pltpu.VMEM((rows, dim), jnp.float32),
            pltpu.VMEM((1, dim), jnp.float32),
            pltpu.VMEM((1, dim), jnp.float32),
            pltpu.VMEM((kv, rows, dim), query_rows.dtype),
            pltpu.VMEM((heads * batch, dim), jnp.float32),
            dma((3,)),
            dma((kv,)),
            dma((kv,)),
            dma((kv,)),
            dma((kv,)),
            dma((devices,)),
            dma((devices,)),
            dma((NX * (NEAR + 2),)),
            dma((kv,)),
            dma((NZ - NEAR - 2,)),
            dma(()),
            pltpu.SemaphoreType.REGULAR,
        ],
        compiler_params=pltpu.CompilerParams(
            collective_id=0, has_side_effects=True, vmem_limit_bytes=40 << 20
        ),
        name="attend",
    )(
        *(
            pltpu.with_memory_space_constraint(a, pltpu.HBM)
            for a in (query_rows, cache_keys, cache_values, page_table.reshape(-1, page), seq_lengths)
        )
    )


def solution(mesh):
    return jax.shard_map(
        shards,
        mesh=mesh,
        in_specs=(
            P("grp", "head", None),
            P(("grp", "seq"), "head", None, None),
            P(("grp", "seq"), "head", None, None),
            P("grp"),
            P("grp"),
        ),
        out_specs=P("grp", "head", None),
        check_vma=False,
    )
```

time: 48.2 us -> 40.7 us (0.84)
  the two profiles are of different devices: /device:TPU:38 before, /device:TPU:40 now
where the time goes in v3:
time: 40.7 us; the launch traced here: 40.6 us
  Pallas kernels  40 us (98%)
  local copies, waits for them, and re-layouts  0.62 us (2%)
    pallas_call x1, Pallas kernels, shards(): pl.pallas_call(kernel, out_shape=jax.ShapeDtypeStruct(query_rows.shape, q...  40 us

profile of v3, /device:TPU:40, one launch (start us, length us, event | category | flops | bytes accessed | tf_op | source)
XLA Modules:
  0.0 40.6 jit_solution(6104707420998078513)
XLA Ops:
  0.0 40.0 %attend.1 = bf16[8,16,128]{2,1,0:T(8,128)(2,1)S(1)} custom-call(bf16[8,16,128]{2,1,0:T(8,128)(2,1)} %q_hbm.1, bf16[32,4,128,128]{3,2,1,0:T(8,128)(2,1)} %k_hbm.1, bf16[32,4,128,128]{3,2,1,0:T(8,128)(2,1)} %v_hbm.1, s32[16,128]{1,0:T(8,128)} %bitcast.1, s32[8]{0:T(128)} %len_hbm.1), custom_call_target="tpu_custom_call" | custom-call | tf_op jit(solution)/shard_map/attend/pallas_call | solution.py:344
  40.0 0.6 %copy.7 = bf16[8,16,128]{2,1,0:T(8,128)(2,1)} copy(bf16[8,16,128]{2,1,0:T(8,128)(2,1)S(1)} %attend.1) | data formatting | bytes 65536

commit v4 on v3

v4 whole, which is shorter than its diff:
```python
import functools
import math

import jax
import jax.numpy as jnp
from jax import lax
from jax.experimental import pallas as pl
from jax.experimental.pallas import tpu as pltpu
from jax.sharding import PartitionSpec as P

MESH = pl.DeviceIdType.MESH
NX, NZ = 4, 16
OWNER = 1
NEAR = 3
RELAY = 5
LATE = 13
VERY_LOW = -1e30
LEVELS = 32767.0


def remote(src, dst, send, recv, seq):
    return pltpu.make_async_remote_copy(
        src_ref=src,
        dst_ref=dst,
        send_sem=send,
        recv_sem=recv,
        device_id={"seq": seq},
        device_id_type=MESH,
    )


def diagonal(rows, lanes, first):
    lane = lax.broadcasted_iota(jnp.int32, (rows, lanes), 1)
    sub = lax.broadcasted_iota(jnp.int32, (rows, lanes), 0)
    return lane == sub + first


def to_column(row, rows):
    return jnp.sum(jnp.where(diagonal(rows, row.shape[1], 0), row, 0.0), axis=1, keepdims=True)


def kernel(
    q_hbm, k_hbm, v_hbm, table_hbm, len_hbm, out_ref,
    len_buf, q_buf, q_f32, k_buf0, k_buf1, v_buf0, v_buf1, table_buf, bias, scores0, scores1, probs0, probs1,
    numer16, stats, recv16, recv_stats, total_numer, total_row, top_row, finished, fin_f32,
    load_sem, k_sem, v_sem, send_p, recv_p, send_f, recv_f, send_w, ready,
):
    slots, kv, page, dim = k_hbm.shape
    batch, heads, _ = q_hbm.shape
    group = heads // kv
    table_rows = table_hbm.shape[0] // batch
    rows = group * batch
    pairs = [(g, g + 1) for g in range(0, kv, 2)]
    devices = NX * NZ

    load_t = pltpu.make_async_copy(table_hbm, table_buf, load_sem.at[0])
    load_l = pltpu.make_async_copy(len_hbm, len_buf, load_sem.at[1])
    load_q = pltpu.make_async_copy(q_hbm, q_buf, load_sem.at[2])
    k_buf, v_buf, scores, probs = (k_buf0, k_buf1), (v_buf0, v_buf1), (scores0, scores1), (probs0, probs1)
    loads_k = [
        pltpu.make_async_copy(k_hbm.at[:, pl.ds(2 * p, 2)], k_buf[p], k_sem.at[p]) for p in range(2)
    ]
    loads_v = [
        pltpu.make_async_copy(v_hbm.at[:, pl.ds(2 * p, 2)], v_buf[p], v_sem.at[p]) for p in range(2)
    ]
    load_t.start()
    load_l.start()
    load_q.start()
    loads_k[0].start()

    me = lax.axis_index("seq")
    x, z = me // NZ, me % NZ
    owner = z == OWNER
    relay = z == RELAY
    fed = jnp.logical_and(z > NEAR, jnp.logical_not(relay))
    owners = [g * NZ + OWNER for g in range(kv)]
    column = [zz for zz in range(NEAR + 1, NZ) if zz != RELAY]

    barrier = pltpu.get_barrier_semaphore()

    def signal(sem, other):
        pl.semaphore_signal(sem, inc=1, device_id={"seq": other}, device_id_type=MESH)

    @pl.when(owner)
    def _():
        @pl.loop(1, devices)
        def _(i):
            signal(barrier, (me + i) % devices)

    @pl.when(jnp.logical_not(owner))
    def _():
        for other in owners:
            signal(barrier, other)

    @pl.when(relay)
    def _():
        for zz in column:
            signal(barrier, x * NZ + zz)

    with jax.named_scope("tw"):
        load_t.wait()
        load_l.wait()
        load_q.wait()
    loads_k[1].start()
    loads_v[0].start()
    loads_v[1].start()
    first = me * slots
    lane = lax.broadcasted_iota(jnp.int32, (batch, page), 1)
    sub = lax.broadcasted_iota(jnp.int32, (batch, page), 0)
    length = jnp.zeros((batch, page), jnp.int32)
    for b in range(batch):
        length = jnp.where(sub == b, len_buf[b], length)
    tables = [table_buf[pl.ds(r, batch, stride=table_rows), :] for r in range(table_rows)]
    spans = [(length - page * (lane + page * r)).astype(jnp.float32) for r in range(table_rows)]
    lane_f32 = lane.astype(jnp.float32)
    for s in range(slots):
        found = functools.reduce(
            jnp.add, [jnp.where(t == first + s, n, 0.0) for t, n in zip(tables, spans)]
        )
        live = jnp.sum(found, axis=1, keepdims=True)
        bias[s] = jnp.where(lane_f32 < live, 0.0, VERY_LOW)
    q_f32[...] = q_buf[...].astype(jnp.float32).reshape(batch * heads, dim)

    factor = math.log2(math.e) / math.sqrt(dim)

    def sends(g):
        slot = z * NX + x
        return (
            remote(numer16.at[g], recv16.at[slot], send_p, recv_p.at[z], owners[g]),
            remote(stats.at[g], recv_stats.at[slot], send_p, recv_p.at[z], owners[g]),
        )

    def wait_for(sem, chunks):
        part = recv_stats.at[pl.ds(0, chunks * (rows // 2 + 1))]
        pltpu.make_async_copy(part, part, sem).wait()

    def wait_rows(sem, chunks):
        part = recv16.at[pl.ds(0, chunks)]
        pltpu.make_async_copy(part, part, sem).wait()

    def queries(p):
        blocks = []
        for i, g in enumerate(pairs[p]):
            query = jnp.concatenate(
                [q_f32[pl.ds(group * g + j, batch, stride=heads), :] for j in range(group)], axis=0
            ).astype(jnp.bfloat16)
            empty = jnp.zeros_like(query)
            blocks.append(jnp.concatenate([empty] * i + [query] + [empty] * (1 - i), axis=1))
        return jnp.concatenate(blocks, axis=0)

    def both(buf, s):
        return jnp.concatenate([buf[s : s + 2, i].reshape(2 * page, dim) for i in range(2)], axis=1)

    def score(p, query, s, best):
        got = lax.dot_general(
            query, both(k_buf[p], s), (((1,), (1,)), ((), ())), preferred_element_type=jnp.float32
        )
        for u in range(2):
            add = jnp.concatenate([bias[s + u]] * (2 * group), axis=0)
            now = got[:, u * page : (u + 1) * page] * factor + add
            scores[p][:, (s + u) * page : (s + u + 1) * page] = now
            best = now if best is None else jnp.maximum(best, now)
        return best

    def weigh(p, top, s, total):
        for u in range(s, s + 2):
            w = jnp.exp2(scores[p][:, u * page : (u + 1) * page] - top)
            total = w if total is None else total + w
            probs[p][:, u * page : (u + 1) * page] = w.astype(jnp.bfloat16)
        return total

    def attend(p, s, numers):
        now = jnp.dot(
            probs[p][:, s * page : (s + 2) * page], both(v_buf[p], s), preferred_element_type=jnp.float32
        )
        return now if numers is None else numers + now

    def finish(p, numers, top, total):
        total = jnp.sum(total, axis=1, keepdims=True)
        for i, g in enumerate(pairs[p]):
            own = slice(i * rows, (i + 1) * rows)
            numer = numers[own, i * dim : (i + 1) * dim]
            largest = jnp.max(jnp.abs(numer), axis=1, keepdims=True)
            steps = numer * (LEVELS / jnp.maximum(largest, 1e-30))
            numer16[g] = jnp.floor(steps + 0.5).astype(jnp.int32).astype(jnp.int16)
            row = sum(
                jnp.where(diagonal(rows, dim, j * rows), c, 0.0)
                for j, c in enumerate((top[own], total[own], largest * (1.0 / LEVELS)))
            )
            stats[g] = jnp.sum(row, axis=0, keepdims=True)

        @pl.when(jnp.logical_not(owner))
        def _():
            with jax.named_scope(f"snd{p}"):
                for g in pairs[p]:
                    for c in sends(g):
                        c.start()

    steps = range(0, slots, 2)
    query0, query1 = queries(0), queries(1)
    with jax.named_scope("kw0"):
        loads_k[0].wait()
    best0 = None
    for s in steps:
        best0 = score(0, query0, s, best0)
    top0 = jnp.max(best0, axis=1, keepdims=True)
    with jax.named_scope("kw1"):
        loads_k[1].wait()
    best1, total0 = None, None
    for s in steps:
        best1 = score(1, query1, s, best1)
        total0 = weigh(0, top0, s, total0)
    top1 = jnp.max(best1, axis=1, keepdims=True)

    with jax.named_scope("bw"):

        @pl.when(fed)
        def _():
            pl.semaphore_wait(barrier, kv + 1)
            signal(ready, x * NZ + RELAY)

        @pl.when(jnp.logical_not(jnp.logical_or(owner, fed)))
        def _():
            pl.semaphore_wait(barrier, kv)

    with jax.named_scope("vw0"):
        loads_v[0].wait()
    numers0, total1 = None, None
    for s in steps:
        numers0 = attend(0, s, numers0)
        total1 = weigh(1, top1, s, total1)
    finish(0, numers0, top0, total0)
    with jax.named_scope("vw1"):
        loads_v[1].wait()
    numers1 = None
    for s in steps:
        numers1 = attend(1, s, numers1)
    finish(1, numers1, top1, total1)

    def near(zz, xx):
        other = xx * NZ + zz
        return remote(
            finished.at[x], finished.at[x], send_f, recv_f, other
        )

    near_z = [*range(NEAR + 1), RELAY]

    @pl.when(owner)
    def _():
        with jax.named_scope("bar"):
            pl.semaphore_wait(barrier, devices - 1)
        for g in range(kv):

            @pl.when(x != g)
            def _():
                for c in sends(g):
                    c.start()

        slot = z * NX + x
        recv16[slot] = numer16[x]
        recv_stats[slot] = stats[x]
        total_numer[...] = jnp.zeros_like(total_numer)
        total_row[...] = jnp.zeros_like(total_row)
        top_row[...] = jnp.full_like(top_row, VERY_LOW)

        def add(zz, chunks=NX):
            sources = [zz * NX + xx for xx in range(NX)]
            with jax.named_scope("rw"):
                wait_for(recv_p.at[zz], chunks)

            got = jnp.concatenate([recv_stats[src] for src in sources] * 2, axis=0)
            totals = pltpu.roll(got, dim - rows, 1)
            scales = pltpu.roll(got, dim - 2 * rows, 1)
            before = top_row[...]
            top = jnp.maximum(before, jnp.max(got, axis=0, keepdims=True))
            weight = jnp.exp2(got - top)
            keep = jnp.exp2(before - top)
            top_row[...] = top
            weighted = weight * totals
            new_total = total_row[...] * keep
            for i in range(NX):
                new_total = new_total + weighted[i : i + 1]
            total_row[...] = new_total
            scaled = weight * scales
            numer = total_numer[...] * to_column(keep, rows)
            for i, src in enumerate(sources):
                numer = numer + recv16[src].astype(jnp.int32).astype(jnp.float32) * to_column(
                    scaled[i : i + 1], rows
                )
            total_numer[...] = numer

        @pl.loop(OWNER + 1, LATE)
        def _(zz):
            add(zz)

        add(OWNER, NX - 1)
        add(0)

        @pl.loop(LATE, NZ)
        def _(zz):
            add(zz)

        done = total_numer[...] / to_column(total_row[...], rows)
        finished[x] = done.astype(finished.dtype)
        with jax.named_scope("bcast"):
            for zz in near_z:
                for xx in range(NX):
                    if zz == OWNER:

                        @pl.when(x != xx)
                        def _():
                            near(zz, xx).start()
                    else:
                        near(zz, xx).start()

    def forward(i):
        return remote(finished, finished, send_w, recv_f, x * NZ + column[i])

    with jax.named_scope("fw"):

        @pl.when(owner)
        def _():
            wait_rows(recv_f, kv - 1)

        @pl.when(jnp.logical_not(owner))
        def _():
            wait_rows(recv_f, kv)

    @pl.when(relay)
    def _():
        pl.semaphore_wait(ready, len(column))
        for i in range(len(column)):
            forward(i).start()

    fin_f32[...] = finished[...].astype(jnp.float32).reshape(heads * batch, dim)
    for b in range(batch):
        out_ref[b] = fin_f32[pl.ds(b, heads, stride=batch), :].astype(out_ref.dtype)

    with jax.named_scope("ws"):

        @pl.when(owner)
        def _():
            wait_for(send_p, kv - 1)
            wait_rows(send_f, len(near_z) * NX - 1)

        @pl.when(jnp.logical_not(owner))
        def _():
            wait_for(send_p, kv)

        @pl.when(relay)
        def _():
            wait_rows(send_w, len(column) * kv)


def shards(query_rows, cache_keys, cache_values, page_table, seq_lengths):
    slots, kv, page, dim = cache_keys.shape
    batch, heads, _ = query_rows.shape
    rows = heads // kv * batch
    devices = NX * NZ
    dma = pltpu.SemaphoreType.DMA
    return pl.pallas_call(
        kernel,
        out_shape=jax.ShapeDtypeStruct(query_rows.shape, query_rows.dtype),
        in_specs=[pl.BlockSpec(memory_space=pltpu.HBM)] * 5,
        out_specs=pl.BlockSpec(memory_space=pltpu.VMEM),
        scratch_shapes=[
            pltpu.SMEM(seq_lengths.shape, seq_lengths.dtype),
            pltpu.VMEM(query_rows.shape, query_rows.dtype),
            pltpu.VMEM((batch * heads, dim), jnp.float32),
            pltpu.VMEM((slots, 2, page, dim), cache_keys.dtype),
            pltpu.VMEM((slots, 2, page, dim), cache_keys.dtype),
            pltpu.VMEM((slots, 2, page, dim), cache_values.dtype),
            pltpu.VMEM((slots, 2, page, dim), cache_values.dtype),
            pltpu.VMEM((page_table.shape[0] // page, page), jnp.int32),
            pltpu.VMEM((slots, batch, page), jnp.float32),
            pltpu.VMEM((2 * rows, slots * page), jnp.float32),
            pltpu.VMEM((2 * rows, slots * page), jnp.float32),
            pltpu.VMEM((2 * rows, slots * page), jnp.bfloat16),
            pltpu.VMEM((2 * rows, slots * page), jnp.bfloat16),
            pltpu.VMEM((kv, rows, dim), jnp.int16),
            pltpu.VMEM((kv, 1, dim), jnp.float32),
            pltpu.VMEM((devices, rows, dim), jnp.int16),
            pltpu.VMEM((NX * (rows // 2 + 1), 1, dim), jnp.float32),
            pltpu.VMEM((rows, dim), jnp.float32),
            pltpu.VMEM((1, dim), jnp.float32),
            pltpu.VMEM((1, dim), jnp.float32),
            pltpu.VMEM((kv, rows, dim), query_rows.dtype),
            pltpu.VMEM((heads * batch, dim), jnp.float32),
            dma((3,)),
            dma((2,)),
            dma((2,)),
            dma(()),
            dma((NZ,)),
            dma(()),
            dma(()),
            dma(()),
            pltpu.SemaphoreType.REGULAR,
        ],
        compiler_params=pltpu.CompilerParams(
            collective_id=0, has_side_effects=True, vmem_limit_bytes=40 << 20
        ),
        name="attend",
    )(
        *(
            pltpu.with_memory_space_constraint(a, pltpu.HBM)
            for a in (query_rows, cache_keys, cache_values, page_table.reshape(-1, page), seq_lengths)
        )
    )


def solution(mesh):
    return jax.shard_map(
        shards,
        mesh=mesh,
        in_specs=(
            P("grp", "head", None),
            P(("grp", "seq"), "head", None, None),
            P(("grp", "seq"), "head", None, None),
            P("grp"),
            P("grp"),
        ),
        out_specs=P("grp", "head", None),
        check_vma=False,
    )
```

time: 40.7 us -> 39.4 us (0.968)
  Pallas kernels: 40 us -> 38.6 us
    pallas_call x1, Pallas kernels: 40 us -> 38.6 us  [shards(): pl.pallas_call(kernel, out_shape=jax.ShapeDtypeStruct(query_rows.shape, q...]
where the time goes in v4:
time: 39.4 us; the launch traced here: 39.2 us
  Pallas kernels  38.6 us (98%)
  local copies, waits for them, and re-layouts  0.62 us (2%)
    pallas_call x1, Pallas kernels, shards(): pl.pallas_call(kernel, out_shape=jax.ShapeDtypeStruct(query_rows.shape, q...  38.6 us

profile of v4, /device:TPU:40, one launch (start us, length us, event | category | flops | bytes accessed | tf_op | source)
XLA Modules:
  0.0 39.2 jit_solution(9266001971429992426)
XLA Ops:
  0.0 38.6 %attend.1 = bf16[8,16,128]{2,1,0:T(8,128)(2,1)S(1)} custom-call(bf16[8,16,128]{2,1,0:T(8,128)(2,1)} %q_hbm.1, bf16[32,4,128,128]{3,2,1,0:T(8,128)(2,1)} %k_hbm.1, bf16[32,4,128,128]{3,2,1,0:T(8,128)(2,1)} %v_hbm.1, s32[16,128]{1,0:T(8,128)} %bitcast.1, s32[8]{0:T(128)} %len_hbm.1), custom_call_target="tpu_custom_call" | custom-call | tf_op jit(solution)/shard_map/attend/pallas_call | solution.py:361
  38.6 0.6 %copy.7 = bf16[8,16,128]{2,1,0:T(8,128)(2,1)} copy(bf16[8,16,128]{2,1,0:T(8,128)(2,1)S(1)} %attend.1) | data formatting | bytes 65536

commit v5 on v4

--- a/solution.py
+++ b/solution.py
@@ -15,6 +15,7 @@
 RELAY = 5
 LATE = 13
 VERY_LOW = -1e30
+LOWEST = -3e38
 LEVELS = 32767.0
 
 
@@ -57,16 +58,27 @@
     load_l = pltpu.make_async_copy(len_hbm, len_buf, load_sem.at[1])
     load_q = pltpu.make_async_copy(q_hbm, q_buf, load_sem.at[2])
     k_buf, v_buf, scores, probs = (k_buf0, k_buf1), (v_buf0, v_buf1), (scores0, scores1), (probs0, probs1)
-    loads_k = [
-        pltpu.make_async_copy(k_hbm.at[:, pl.ds(2 * p, 2)], k_buf[p], k_sem.at[p]) for p in range(2)
-    ]
-    loads_v = [
-        pltpu.make_async_copy(v_hbm.at[:, pl.ds(2 * p, 2)], v_buf[p], v_sem.at[p]) for p in range(2)
-    ]
+    half = slots // 2
+
+    def loads(source, target, p, sems, parts):
+        size = slots // parts
+        return [
+            pltpu.make_async_copy(
+                source.at[pl.ds(i * size, size), pl.ds(2 * p, 2)], target.at[pl.ds(i * size, size)], sems.at[i]
+            )
+            for i in range(parts)
+        ]
+
+    loads_k0 = loads(k_hbm, k_buf0, 0, k_sem.at[pl.ds(0, 2)], 2)
+    loads_k1 = loads(k_hbm, k_buf1, 1, k_sem.at[pl.ds(2, 1)], 1)
+    loads_v0 = loads(v_hbm, v_buf0, 0, v_sem.at[pl.ds(0, 1)], 1)
+    loads_v1 = loads(v_hbm, v_buf1, 1, v_sem.at[pl.ds(1, 2)], 2)
+
     load_t.start()
     load_l.start()
     load_q.start()
-    loads_k[0].start()
+    for c in loads_k0:
+        c.start()
 
     me = lax.axis_index("seq")
     x, z = me // NZ, me % NZ
@@ -101,9 +113,7 @@
         load_t.wait()
         load_l.wait()
         load_q.wait()
-    loads_k[1].start()
-    loads_v[0].start()
-    loads_v[1].start()
+    loads_v0[0].start()
     first = me * slots
     lane = lax.broadcasted_iota(jnp.int32, (batch, page), 1)
     sub = lax.broadcasted_iota(jnp.int32, (batch, page), 0)
@@ -173,7 +183,11 @@
         now = jnp.dot(
             probs[p][:, s * page : (s + 2) * page], both(v_buf[p], s), preferred_element_type=jnp.float32
         )
-        return now if numers is None else numers + now
+        turn = s // 2 % 2
+        numers[turn] = now if numers[turn] is None else numers[turn] + now
+
+    def joined(sums):
+        return jnp.maximum(sums[0], LOWEST) + sums[1]
 
     def finish(p, numers, top, total):
         total = jnp.sum(total, axis=1, keepdims=True)
@@ -198,44 +212,50 @@
 
     steps = range(0, slots, 2)
     query0, query1 = queries(0), queries(1)
-    with jax.named_scope("kw0"):
-        loads_k[0].wait()
     best0 = None
+    for i in range(2):
+        with jax.named_scope(f"kw0{i}"):
+            loads_k0[i].wait()
+        if i == 1:
+            loads_k1[0].start()
+        for s in range(i * half, (i + 1) * half, 2):
+            best0 = score(0, query0, s, best0)
+    top0 = jnp.max(best0, axis=1, keepdims=True)
+    with jax.named_scope("vw0"):
+        loads_v0[0].wait()
+    for c in loads_v1:
+        c.start()
+    numers0, total0 = [None, None], None
     for s in steps:
-        best0 = score(0, query0, s, best0)
-    top0 = jnp.max(best0, axis=1, keepdims=True)
+        total0 = weigh(0, top0, s, total0)
+        attend(0, s, numers0)
+
+    with jax.named_scope("bw"):
+
+        @pl.when(fed)
+        def _():
+            pl.semaphore_wait(barrier, kv + 1)
+            signal(ready, x * NZ + RELAY)
+
+        @pl.when(jnp.logical_not(jnp.logical_or(owner, fed)))
+        def _():
+            pl.semaphore_wait(barrier, kv)
+
+    finish(0, joined(numers0), top0, total0)
     with jax.named_scope("kw1"):
-        loads_k[1].wait()
-    best1, total0 = None, None
+        loads_k1[0].wait()
+    best1 = None
     for s in steps:
         best1 = score(1, query1, s, best1)
-        total0 = weigh(0, top0, s, total0)
     top1 = jnp.max(best1, axis=1, keepdims=True)
-
-    with jax.named_scope("bw"):
-
-        @pl.when(fed)
-        def _():
-            pl.semaphore_wait(barrier, kv + 1)
-            signal(ready, x * NZ + RELAY)
-
-        @pl.when(jnp.logical_not(jnp.logical_or(owner, fed)))
-        def _():
-            pl.semaphore_wait(barrier, kv)
-
-    with jax.named_scope("vw0"):
-        loads_v[0].wait()
-    numers0, total1 = None, None
-    for s in steps:
-        numers0 = attend(0, s, numers0)
-        total1 = weigh(1, top1, s, total1)
-    finish(0, numers0, top0, total0)
-    with jax.named_scope("vw1"):
-        loads_v[1].wait()
-    numers1 = None
-    for s in steps:
-        numers1 = attend(1, s, numers1)
-    finish(1, numers1, top1, total1)
+    numers1, total1 = [None, None], None
+    for i in range(2):
+        with jax.named_scope(f"vw1{i}"):
+            loads_v1[i].wait()
+        for s in range(i * half, (i + 1) * half, 2):
+            total1 = weigh(1, top1, s, total1)
+            attend(1, s, numers1)
+    finish(1, joined(numers1), top1, total1)
 
     def near(zz, xx):
         other = xx * NZ + zz
@@ -387,8 +407,8 @@
             pltpu.VMEM((kv, rows, dim), query_rows.dtype),
             pltpu.VMEM((heads * batch, dim), jnp.float32),
             dma((3,)),
-            dma((2,)),
-            dma((2,)),
+            dma((3,)),
+            dma((3,)),
             dma(()),
             dma((NZ,)),
             dma(()),

time: 39.4 us -> 37.8 us (0.959)
  Pallas kernels: 38.6 us -> 37.1 us
    pallas_call x1, Pallas kernels: 38.6 us -> 37.1 us  [shards(): pl.pallas_call(kernel, out_shape=jax.ShapeDtypeStruct(query_rows.shape, q...]
where the time goes in v5:
time: 37.8 us; the launch traced here: 37.7 us
  Pallas kernels  37.1 us (98%)
  local copies, waits for them, and re-layouts  0.62 us (2%)
    pallas_call x1, Pallas kernels, shards(): pl.pallas_call(kernel, out_shape=jax.ShapeDtypeStruct(query_rows.shape, q...  37.1 us

profile of v5, /device:TPU:40, one launch (start us, length us, event | category | flops | bytes accessed | tf_op | source)
XLA Modules:
  0.0 37.7 jit_solution(14732891794352474054)
XLA Ops:
  0.0 37.1 %attend.1 = bf16[8,16,128]{2,1,0:T(8,128)(2,1)S(1)} custom-call(bf16[8,16,128]{2,1,0:T(8,128)(2,1)} %q_hbm.1, bf16[32,4,128,128]{3,2,1,0:T(8,128)(2,1)} %k_hbm.1, bf16[32,4,128,128]{3,2,1,0:T(8,128)(2,1)} %v_hbm.1, s32[16,128]{1,0:T(8,128)} %bitcast.1, s32[8]{0:T(128)} %len_hbm.1), custom_call_target="tpu_custom_call" | custom-call | tf_op jit(solution)/shard_map/attend/pallas_call | solution.py:381
  37.1 0.6 %copy.7 = bf16[8,16,128]{2,1,0:T(8,128)(2,1)} copy(bf16[8,16,128]{2,1,0:T(8,128)(2,1)S(1)} %attend.1) | data formatting | bytes 65536

commit v6 on v5

--- a/solution.py
+++ b/solution.py
@@ -77,8 +77,9 @@
     load_t.start()
     load_l.start()
     load_q.start()
-    for c in loads_k0:
-        c.start()
+    loads_k0[0].start()
+    loads_k0[1].start()
+    loads_v0[0].start()
 
     me = lax.axis_index("seq")
     x, z = me // NZ, me % NZ
@@ -113,7 +114,7 @@
         load_t.wait()
         load_l.wait()
         load_q.wait()
-    loads_v0[0].start()
+    loads_k1[0].start()
     first = me * slots
     lane = lax.broadcasted_iota(jnp.int32, (batch, page), 1)
     sub = lax.broadcasted_iota(jnp.int32, (batch, page), 0)
@@ -216,15 +217,14 @@
     for i in range(2):
         with jax.named_scope(f"kw0{i}"):
             loads_k0[i].wait()
-        if i == 1:
-            loads_k1[0].start()
+        if i == 0:
+            loads_v1[0].start()
+            loads_v1[1].start()
         for s in range(i * half, (i + 1) * half, 2):
             best0 = score(0, query0, s, best0)
     top0 = jnp.max(best0, axis=1, keepdims=True)
     with jax.named_scope("vw0"):
         loads_v0[0].wait()
-    for c in loads_v1:
-        c.start()
     numers0, total0 = [None, None], None
     for s in steps:
         total0 = weigh(0, top0, s, total0)

time: 37.8 us -> 37.3 us (0.987)
  Pallas kernels: 37.1 us -> 36.6 us
    pallas_call x1, Pallas kernels: 37.1 us -> 36.6 us  [shards(): pl.pallas_call(kernel, out_shape=jax.ShapeDtypeStruct(query_rows.shape, q...]
where the time goes in v6:
time: 37.3 us; the launch traced here: 37.2 us
  Pallas kernels  36.6 us (98%)
  local copies, waits for them, and re-layouts  0.62 us (2%)
    pallas_call x1, Pallas kernels, shards(): pl.pallas_call(kernel, out_shape=jax.ShapeDtypeStruct(query_rows.shape, q...  36.6 us

profile of v6, /device:TPU:40, one launch (start us, length us, event | category | flops | bytes accessed | tf_op | source)
XLA Modules:
  0.0 37.2 jit_solution(5671303833017403117)
XLA Ops:
  0.0 36.6 %attend.1 = bf16[8,16,128]{2,1,0:T(8,128)(2,1)S(1)} custom-call(bf16[8,16,128]{2,1,0:T(8,128)(2,1)} %q_hbm.1, bf16[32,4,128,128]{3,2,1,0:T(8,128)(2,1)} %k_hbm.1, bf16[32,4,128,128]{3,2,1,0:T(8,128)(2,1)} %v_hbm.1, s32[16,128]{1,0:T(8,128)} %bitcast.1, s32[8]{0:T(128)} %len_hbm.1), custom_call_target="tpu_custom_call" | custom-call | tf_op jit(solution)/shard_map/attend/pallas_call | solution.py:381
  36.6 0.6 %copy.7 = bf16[8,16,128]{2,1,0:T(8,128)(2,1)} copy(bf16[8,16,128]{2,1,0:T(8,128)(2,1)S(1)} %attend.1) | data formatting | bytes 65536

commit v7 on v6

--- a/solution.py
+++ b/solution.py
@@ -213,6 +213,17 @@
 
     steps = range(0, slots, 2)
     query0, query1 = queries(0), queries(1)
+    with jax.named_scope("bw"):
+
+        @pl.when(fed)
+        def _():
+            pl.semaphore_wait(barrier, kv + 1)
+            signal(ready, x * NZ + RELAY)
+
+        @pl.when(jnp.logical_not(jnp.logical_or(owner, fed)))
+        def _():
+            pl.semaphore_wait(barrier, kv)
+
     best0 = None
     for i in range(2):
         with jax.named_scope(f"kw0{i}"):
@@ -229,17 +240,6 @@
     for s in steps:
         total0 = weigh(0, top0, s, total0)
         attend(0, s, numers0)
-
-    with jax.named_scope("bw"):
-
-        @pl.when(fed)
-        def _():
-            pl.semaphore_wait(barrier, kv + 1)
-            signal(ready, x * NZ + RELAY)
-
-        @pl.when(jnp.logical_not(jnp.logical_or(owner, fed)))
-        def _():
-            pl.semaphore_wait(barrier, kv)
 
     finish(0, joined(numers0), top0, total0)
     with jax.named_scope("kw1"):

time: 37.3 us -> 37.3 us (level)
  no operation moved by 1% of the time
where the time goes in v7:
time: 37.3 us; the launch traced here: 37.2 us
  Pallas kernels  36.6 us (98%)
  local copies, waits for them, and re-layouts  0.62 us (2%)
    pallas_call x1, Pallas kernels, shards(): pl.pallas_call(kernel, out_shape=jax.ShapeDtypeStruct(query_rows.shape, q...  36.6 us

profile of v7, /device:TPU:40, one launch (start us, length us, event | category | flops | bytes accessed | tf_op | source)
XLA Modules:
  0.0 37.2 jit_solution(2358278478559443579)
XLA Ops:
  0.0 36.6 %attend.1 = bf16[8,16,128]{2,1,0:T(8,128)(2,1)S(1)} custom-call(bf16[8,16,128]{2,1,0:T(8,128)(2,1)} %q_hbm.1, bf16[32,4,128,128]{3,2,1,0:T(8,128)(2,1)} %k_hbm.1, bf16[32,4,128,128]{3,2,1,0:T(8,128)(2,1)} %v_hbm.1, s32[16,128]{1,0:T(8,128)} %bitcast.1, s32[8]{0:T(128)} %len_hbm.1), custom_call_target="tpu_custom_call" | custom-call | tf_op jit(solution)/shard_map/attend/pallas_call | solution.py:381
  36.6 0.6 %copy.7 = bf16[8,16,128]{2,1,0:T(8,128)(2,1)} copy(bf16[8,16,128]{2,1,0:T(8,128)(2,1)S(1)} %attend.1) | data formatting | bytes 65536

commit v8 on v6

--- a/solution.py
+++ b/solution.py
@@ -207,7 +207,7 @@
         @pl.when(jnp.logical_not(owner))
         def _():
             with jax.named_scope(f"snd{p}"):
-                for g in pairs[p]:
+                for g in pairs[p] if p else pairs[p][::-1]:
                     for c in sends(g):
                         c.start()
 

time: 37.3 us -> 37.3 us (level)
  no operation moved by 1% of the time
where the time goes in v8:
time: 37.3 us; the launch traced here: 37.2 us
  Pallas kernels  36.6 us (98%)
  local copies, waits for them, and re-layouts  0.62 us (2%)
    pallas_call x1, Pallas kernels, shards(): pl.pallas_call(kernel, out_shape=jax.ShapeDtypeStruct(query_rows.shape, q...  36.6 us

profile of v8, /device:TPU:40, one launch (start us, length us, event | category | flops | bytes accessed | tf_op | source)
XLA Modules:
  0.0 37.2 jit_solution(10768744306473077075)
XLA Ops:
  0.0 36.6 %attend.1 = bf16[8,16,128]{2,1,0:T(8,128)(2,1)S(1)} custom-call(bf16[8,16,128]{2,1,0:T(8,128)(2,1)} %q_hbm.1, bf16[32,4,128,128]{3,2,1,0:T(8,128)(2,1)} %k_hbm.1, bf16[32,4,128,128]{3,2,1,0:T(8,128)(2,1)} %v_hbm.1, s32[16,128]{1,0:T(8,128)} %bitcast.1, s32[8]{0:T(128)} %len_hbm.1), custom_call_target="tpu_custom_call" | custom-call | tf_op jit(solution)/shard_map/attend/pallas_call | solution.py:381
  36.6 0.6 %copy.7 = bf16[8,16,128]{2,1,0:T(8,128)(2,1)} copy(bf16[8,16,128]{2,1,0:T(8,128)(2,1)S(1)} %attend.1) | data formatting | bytes 65536
